TPU v7x, 32 devices: a whole 2x2x4 slice. The times are simulated.
32 devices in a mesh: dp: 8 (over z, y), tensor: 4 (over x, core).
Axes of the slice: x: 2, y: 2, z: 4, core: 2. Of those that a mesh axis runs over, the one named last changes fastest.
Arguments:
- tokens: bfloat16 [37632, 768], P(('dp', 'tensor')), may hold values from -21 to 21
- res_class: int32 [192], P('dp'), may hold values from 0 to 1
- gain_attn: float32 [768], replicated, may hold values from 0.5 to 1.5
- shift_attn: float32 [768], replicated, may hold values from -1.5 to 1.5
- w_qkv: bfloat16 [768, 3, 768], P(None, None, 'tensor'), may hold values from -0.3125 to 0.3125
- bias_qv: float32 [2, 768], P(None, 'tensor'), may hold values from -1.5 to 1.5
- w_out: bfloat16 [768, 768], P('tensor'), may hold values from -0.625 to 0.625
- bias_out: float32 [768], replicated, may hold values from -1.5 to 1.5
- gain_mlp: float32 [768], replicated, may hold values from 0.5 to 1.5
- shift_mlp: float32 [768], replicated, may hold values from -1.5 to 1.5
- w_up: bfloat16 [768, 3072], P(None, 'tensor'), may hold values from -0.21875 to 0.21875
- bias_up: float32 [3072], P('tensor'), may hold values from -1.5 to 1.5
- w_down: bfloat16 [3072, 768], P('tensor'), may hold values from -0.15625 to 0.15625
- bias_down: float32 [768], replicated, may hold values from -1.5 to 1.5
- cotangent: bfloat16 [37632, 768], P(('dp', 'tensor')), may hold values from -21 to 21
Outputs:
- block_out: bfloat16 [37632, 768], P(('dp', 'tensor'))
- grad_tokens: float32 [37632, 768], P(('dp', 'tensor'))
- grad_gain_attn: float32 [768], replicated
- grad_shift_attn: float32 [768], replicated
- grad_qkv: float32 [768, 3, 768], P(None, None, 'tensor')
- grad_bias_qv: float32 [2, 768], P(None, 'tensor')
- grad_out: float32 [768, 768], P('tensor')
- grad_bias_out: float32 [768], replicated
- grad_gain_mlp: float32 [768], replicated
- grad_shift_mlp: float32 [768], replicated
- grad_up: float32 [768, 3072], P(None, 'tensor')
- grad_bias_up: float32 [3072], P('tensor')
- grad_down: float32 [3072, 768], P('tensor')
- grad_bias_down: float32 [768], replicated
- rms: float32 [3], replicated
All inputs are finite; a program needn't handle non-finite values.
Results may differ from a plain program's by a relative error of at most 0.017.
Values may be sent and summed in bfloat16 or wider, within the bound.
A program may use at most 256 MiB of HBM per device.

v0:
```python
import jax
import jax.numpy as jnp
from jax import lax
from jax.sharding import PartitionSpec as P

HEAD_DIM = 64
PATCHES = 196
PATCHES_LOW = 144


EPS = 1e-06


def normalize(values):
    mean = jnp.mean(values, axis=-1, keepdims=True)
    centred = values - mean
    factor = lax.rsqrt(jnp.mean(centred * centred, axis=-1, keepdims=True) + EPS)
    return (centred * factor, factor)


def norm_back(grad_out, gain, normed, factor):
    scaled = grad_out * gain
    return factor * (
        scaled
        - jnp.mean(scaled, axis=-1, keepdims=True)
        - normed * jnp.mean(scaled * normed, axis=-1, keepdims=True)
    )


def exact_gelu(values):
    return jax.nn.gelu(values, approximate=False)


def on_device(
    tokens,
    res_class,
    gain_attn,
    shift_attn,
    w_qkv,
    bias_qv,
    w_out,
    bias_out,
    gain_mlp,
    shift_mlp,
    w_up,
    bias_up,
    w_down,
    bias_down,
    cotangent,
):
    rows = tokens.shape[0]
    width = tokens.shape[1]
    images = res_class.shape[0]
    local = w_qkv.shape[2]
    heads_here = local // HEAD_DIM
    scale = HEAD_DIM ** (-0.5)
    place = lax.axis_index("tensor")
    counts = jnp.where(res_class == 0, PATCHES, PATCHES_LOW)
    key_valid = jnp.arange(PATCHES)[None, :] < counts[:, None]
    flat_valid = key_valid.reshape(-1).astype(jnp.float32)
    row_valid = lax.dynamic_slice_in_dim(flat_valid, place * rows, rows)[:, None]
    mask = key_valid[:, None, None, :]
    shape = (images, PATCHES, heads_here, HEAD_DIM)
    w_qkv_flat = w_qkv.reshape(width, 3 * local)
    inputs = tokens.astype(jnp.float32)
    normed_a, factor_a = normalize(inputs)
    in_attn = (normed_a * gain_attn + shift_attn).astype(jnp.bfloat16)
    full_attn = lax.all_gather(in_attn, "tensor", axis=0, tiled=True)
    qkv = jnp.dot(full_attn, w_qkv_flat, preferred_element_type=jnp.float32).reshape(-1, 3, local)
    query = (qkv[:, 0] + bias_qv[0]).astype(jnp.bfloat16).reshape(shape)
    keys = qkv[:, 1].astype(jnp.bfloat16).reshape(shape)
    values = (qkv[:, 2] + bias_qv[1]).astype(jnp.bfloat16).reshape(shape)
    scores = jnp.einsum("iqhd,ikhd->ihqk", query, keys, preferred_element_type=jnp.float32) * scale
    scores = jnp.where(mask, scores, -1e30)
    log_total = jax.nn.logsumexp(scores, axis=-1, keepdims=True)
    probs = jnp.exp(scores - log_total).astype(jnp.bfloat16)
    context = (
        jnp.einsum("ihqk,ikhd->iqhd", probs, values, preferred_element_type=jnp.float32)
        .reshape(-1, local)
        .astype(jnp.bfloat16)
    )
    piece = context
    branch = (
        lax.psum_scatter(
            jnp.dot(piece, w_out, preferred_element_type=jnp.float32).astype(jnp.bfloat16),
            "tensor",
            scatter_dimension=0,
            tiled=True,
        ).astype(jnp.float32)
        + bias_out
    )
    hidden = inputs + branch
    normed_m, factor_m = normalize(hidden)
    in_mlp = (normed_m * gain_mlp + shift_mlp).astype(jnp.bfloat16)
    full_mlp = lax.all_gather(in_mlp, "tensor", axis=0, tiled=True)
    pre_act = jnp.dot(full_mlp, w_up, preferred_element_type=jnp.float32) + bias_up
    act = exact_gelu(pre_act).astype(jnp.bfloat16)
    piece = act
    mlp = (
        lax.psum_scatter(
            jnp.dot(piece, w_down, preferred_element_type=jnp.float32).astype(jnp.bfloat16),
            "tensor",
            scatter_dimension=0,
            tiled=True,
        ).astype(jnp.float32)
        + bias_down
    )
    stream = (hidden + mlp) * row_valid
    block_out = stream.astype(jnp.bfloat16)
    grad_stream = cotangent.astype(jnp.float32) * row_valid
    grad_bias_down = jnp.sum(grad_stream, axis=0)
    grad_mlp_full = lax.all_gather(grad_stream.astype(jnp.bfloat16), "tensor", axis=0, tiled=True)
    weight_down = jnp.einsum("tf,td->fd", act, grad_mlp_full, preferred_element_type=jnp.float32)
    grad_act = jnp.einsum("td,fd->tf", grad_mlp_full, w_down, preferred_element_type=jnp.float32)
    gelu_out, gelu_back = jax.vjp(exact_gelu, pre_act)
    grad_pre = gelu_back(grad_act)[0]
    grad_bias_up = jnp.sum(grad_pre, axis=0)
    grad_pre_low = grad_pre.astype(jnp.bfloat16)
    weight_up = jnp.einsum("td,tf->df", full_mlp, grad_pre_low, preferred_element_type=jnp.float32)
    piece = grad_pre_low
    grad_in_mlp = lax.psum_scatter(
        jnp.einsum("tf,df->td", piece, w_up, preferred_element_type=jnp.float32).astype(
            jnp.bfloat16
        ),
        "tensor",
        scatter_dimension=0,
        tiled=True,
    ).astype(jnp.float32)
    grad_gain_mlp = jnp.sum(grad_in_mlp * normed_m, axis=0)
    grad_shift_mlp = jnp.sum(grad_in_mlp, axis=0)
    grad_hidden = grad_stream + norm_back(grad_in_mlp, gain_mlp, normed_m, factor_m)
    grad_bias_out = jnp.sum(grad_hidden, axis=0)
    grad_branch_full = lax.all_gather(
        grad_hidden.astype(jnp.bfloat16), "tensor", axis=0, tiled=True
    )
    weight_out = jnp.einsum(
        "tc,td->cd", context, grad_branch_full, preferred_element_type=jnp.float32
    )
    grad_context = (
        jnp.einsum("td,cd->tc", grad_branch_full, w_out, preferred_element_type=jnp.float32)
        .astype(jnp.bfloat16)
        .reshape(shape)
    )
    again = jnp.einsum("iqhd,ikhd->ihqk", query, keys, preferred_element_type=jnp.float32) * scale
    again = jnp.where(mask, again, -1e30)
    probs_full = jnp.exp(again - log_total)
    probs_low = probs_full.astype(jnp.bfloat16)
    grad_value = jnp.einsum(
        "ihqk,iqhd->ikhd", probs_low, grad_context, preferred_element_type=jnp.float32
    )
    grad_probs = jnp.einsum(
        "iqhd,ikhd->ihqk", grad_context, values, preferred_element_type=jnp.float32
    )
    row_dot = jnp.sum(probs_full * grad_probs, axis=-1, keepdims=True)
    grad_scores = (probs_full * (grad_probs - row_dot)).astype(jnp.bfloat16)
    grad_query = scale * jnp.einsum(
        "ihqk,ikhd->iqhd", grad_scores, keys, preferred_element_type=jnp.float32
    )
    grad_key = scale * jnp.einsum(
        "ihqk,iqhd->ikhd", grad_scores, query, preferred_element_type=jnp.float32
    )
    query_low = grad_query.reshape(-1, local).astype(jnp.bfloat16)
    key_low = grad_key.reshape(-1, local).astype(jnp.bfloat16)
    value_low = grad_value.reshape(-1, local).astype(jnp.bfloat16)
    grad_bias_qv = jnp.stack(
        [
            jnp.sum(query_low.astype(jnp.float32), axis=0),
            jnp.sum(value_low.astype(jnp.float32), axis=0),
        ]
    )
    grad_qkv_low = jnp.stack([query_low, key_low, value_low], axis=1).reshape(-1, 3 * local)
    weight_qkv = jnp.einsum(
        "td,tc->dc", full_attn, grad_qkv_low, preferred_element_type=jnp.float32
    ).reshape(width, 3, local)
    piece = grad_qkv_low
    grad_in_attn = lax.psum_scatter(
        jnp.einsum("tc,dc->td", piece, w_qkv_flat, preferred_element_type=jnp.float32).astype(
            jnp.bfloat16
        ),
        "tensor",
        scatter_dimension=0,
        tiled=True,
    ).astype(jnp.float32)
    grad_gain_attn = jnp.sum(grad_in_attn * normed_a, axis=0)
    grad_shift_attn = jnp.sum(grad_in_attn, axis=0)
    grad_tokens = grad_hidden + norm_back(grad_in_attn, gain_attn, normed_a, factor_a)
    totals = jnp.stack(
        [
            jnp.sum(stream * stream),
            jnp.sum(branch * branch * row_valid),
            jnp.sum(mlp * mlp * row_valid),
            jnp.sum(row_valid),
        ]
    )
    summed = lax.psum(
        (
            grad_gain_attn,
            grad_shift_attn,
            grad_bias_out,
            grad_gain_mlp,
            grad_shift_mlp,
            grad_bias_down,
            totals,
        ),
        ("dp", "tensor"),
    )
    weight_qkv, grad_bias_qv, weight_out, weight_up, grad_bias_up, weight_down = lax.psum(
        (weight_qkv, grad_bias_qv, weight_out, weight_up, grad_bias_up, weight_down), "dp"
    )
    sums = summed[6]
    rms = jnp.sqrt(sums[:3] / (sums[3] * width))
    return (
        block_out,
        grad_tokens,
        summed[0],
        summed[1],
        weight_qkv,
        grad_bias_qv,
        weight_out,
        summed[2],
        summed[3],
        summed[4],
        weight_up,
        grad_bias_up,
        weight_down,
        summed[5],
        rms,
    )


def solution(mesh):
    in_specs = (
        P(("dp", "tensor"), None),
        P("dp"),
        P(),
        P(),
        P(None, None, "tensor"),
        P(None, "tensor"),
        P("tensor", None),
        P(),
        P(),
        P(),
        P(None, "tensor"),
        P("tensor"),
        P("tensor", None),
        P(),
        P(("dp", "tensor"), None),
    )
    out_specs = (
        P(("dp", "tensor"), None),
        P(("dp", "tensor"), None),
        P(),
        P(),
        P(None, None, "tensor"),
        P(None, "tensor"),
        P("tensor", None),
        P(),
        P(),
        P(),
        P(None, "tensor"),
        P("tensor"),
        P("tensor", None),
        P(),
        P(),
    )
    return jax.shard_map(
        on_device, mesh=mesh, in_specs=in_specs, out_specs=out_specs, check_vma=False
    )
```

profile of v0, /device:TPU:0, one launch (start us, length us, event | category | flops | bytes accessed | tf_op | source)
XLA Modules:
  0.0 985.5 jit_solution(16900257428672392909)
XLA Ops:
  16.8 52.4 %all-gather.5.cloned.1.call-done = bf16[4704,768]{1,0:T(8,128)(2,1)} async-done(((bf16[1176,768]{1,0:T(8,128)(2,1)}), bf16[4704,768]{1,0:T(8,128)(2,1)}) %all-gather.5.cloned.1.call-update) | async-done | bytes 7225360 | tf_op jit(solution)/shard_map/all_gather | solution.py:68
  69.2 7.3 fusion.10
  77.9 3.4 fusion.73
  81.4 6.0 convert_element_type.155
  87.4 6.4 squeeze.9
  93.9 6.4 squeeze.8
  100.3 7.4 fusion.6
  108.3 4.4 exponential_reduce_fusion
  113.8 11.1 %convert_bitcast_fusion = bf16[24,196,3,64]{1,3,2,0:T(8,128)(2,1)S(1)} fusion(f32[24,196,3,64]{1,0,3,2:T(8,128)} %squeeze.8, f32[3,64]{1,0:T(4,128)} %add.138, f32[24,3,196,196]{2,3,1,0:T(8,128)} %copy-done.2, f32[24,3,196]{2,1,0:T(4,128)S(1)} %log_add_fusion, pred[24,196]{1,0:T(8,128)(4,1)S(1)} %get-tuple-element.54), kind=kOutput, calls=%fused_computation.91 | convolution fusion | flops 367815168 | bytes 16544736 | tf_op jit(solution)/shard_map/ihqk,ikhd->iqhd/dot_general | solution.py:78
  127.7 4.7 convert_element_type.159
  132.4 6.5 convolution_convert_fusion.2
  140.5 63.8 %reduce-scatter.5.cloned.1.call-done = bf16[1176,768]{1,0:T(8,128)(2,1)} async-done(((bf16[4704,768]{1,0:T(8,128)(2,1)}), bf16[1176,768]{1,0:T(8,128)(2,1)}) %reduce-scatter.5.cloned.1.call-update) | async-done | bytes 1806352 | tf_op jit(solution)/shard_map/reduce_scatter | solution.py:84
  206.9 5.1 multiply_reduce_fusion.2
  215.5 51.2 %all-gather.7.cloned.1.call-done = bf16[4704,768]{1,0:T(8,128)(2,1)} async-done(((bf16[1176,768]{1,0:T(8,128)(2,1)}), bf16[4704,768]{1,0:T(8,128)(2,1)}) %all-gather.7.cloned.1.call-update) | async-done | bytes 7225360 | tf_op jit(solution)/shard_map/all_gather | solution.py:95
  266.7 11.9 %fusion.74 = f32[4704,768]{1,0:T(8,128)} fusion(bf16[4704,768]{1,0:T(8,128)(2,1)} %all-gather.7.cloned.1.call-done, bf16[768,768]{1,0:T(8,128)(2,1)} %param.25), kind=kOutput, calls=%fused_computation.132 | convolution fusion | flops 5549064192 | bytes 22855680 | tf_op jit(solution)/shard_map/dot_general | solution.py:96
  278.6 41.8 %all-gather.9.cloned.1.call-done = bf16[4704,768]{1,0:T(8,128)(2,1)} async-done(((bf16[1176,768]{1,0:T(8,128)(2,1)}), bf16[4704,768]{1,0:T(8,128)(2,1)}) %all-gather.9.cloned.1.call-update) | async-done | bytes 7225360 | tf_op jit(solution)/shard_map/all_gather | solution.py:112
  320.4 41.1 %fusion.68 = (f32[768]{0:T(1024)S(1)}, bf16[4704,768]{1,0:T(8,128)(2,1)}, f32[4704,768]{1,0:T(8,128)S(1)}) fusion(f32[4704,768]{1,0:T(8,128)} %fusion.74, f32[768]{0:T(1024)S(1)} %copy-done.50, bf16[4704,768]{1,0:T(8,128)(2,1)} %all-gather.9.cloned.1.call-done, bf16[768,768]{1,0:T(8,128)(2,1)S(1)} %copy-done), kind=kOutput, calls=%fused_computation.128 | convolution fusion | flops 5816400896 | bytes 44537856 | tf_op jit(solution)/shard_map/td,fd->tf/dot_general | solution.py:114
  361.5 4.3 multiply_convert_fusion.1
  365.8 10.8 %convolution_convert_fusion.1 = bf16[4704,768]{1,0:T(8,128)(2,1)} fusion(bf16[4704,768]{1,0:T(8,128)(2,1)} %multiply_convert_fusion.1, bf16[768,768]{1,0:T(8,128)(2,1)S(1)} %copy-done), kind=kOutput, calls=%fused_computation.25 | convolution fusion | flops 5552676864 | bytes 15630336 | tf_op jit(solution)/shard_map/dot_general | solution.py:101
  377.9 11.0 %convolution_convert_fusion = bf16[4704,768]{1,0:T(8,128)(2,1)} fusion(bf16[768,768]{1,0:T(8,128)(2,1)S(1)} %copy-done.54, bf16[4704,768]{1,0:T(8,128)(2,1)} %get-tuple-element.43), kind=kOutput, calls=%fused_computation.24 | convolution fusion | flops 5552676864 | bytes 15630336 | tf_op jit(solution)/shard_map/tf,df->td/dot_general | solution.py:122
  389.0 53.0 %reduce-scatter.7.cloned.1.call-done = bf16[1176,768]{1,0:T(8,128)(2,1)} async-done(((bf16[4704,768]{1,0:T(8,128)(2,1)}), bf16[1176,768]{1,0:T(8,128)(2,1)}) %reduce-scatter.7.cloned.1.call-update) | async-done | bytes 1806352 | tf_op jit(solution)/shard_map/reduce_scatter | solution.py:100
  442.0 67.6 %reduce-scatter.9.cloned.1.call-done = bf16[1176,768]{1,0:T(8,128)(2,1)} async-done(((bf16[4704,768]{1,0:T(8,128)(2,1)}), bf16[1176,768]{1,0:T(8,128)(2,1)}) %reduce-scatter.9.cloned.1.call-update) | async-done | bytes 1806352 | tf_op jit(solution)/shard_map/reduce_scatter | solution.py:121
  509.6 8.3 fusion.36
  523.6 51.8 %all-gather.11.cloned.1.call-done = bf16[4704,768]{1,0:T(8,128)(2,1)} async-done(((bf16[1176,768]{1,0:T(8,128)(2,1)}), bf16[4704,768]{1,0:T(8,128)(2,1)}) %all-gather.11.cloned.1.call-update) | async-done | bytes 7225360 | tf_op jit(solution)/shard_map/all_gather | solution.py:133
  575.4 6.8 convolution_convert_fusion.3
  582.2 6.2 reshape.193
  588.4 9.9 %convert_reduce_fusion.3 = (f32[3,64]{1,0:T(4,128)S(1)}, bf16[24,3,64,196]{3,2,1,0:T(8,128)(2,1)}) fusion(f32[24,3,196,196]{2,3,1,0:T(8,128)} %copy-done.2, f32[24,3,196]{2,1,0:T(4,128)S(1)} %copy-done.24, pred[24,196]{1,0:T(8,128)(4,1)S(1)} %copy-done.30, bf16[24,196,3,64]{1,0,3,2:T(8,128)(2,1)} %reshape.193), kind=kOutput, calls=%fused_computation.53 | convolution fusion | flops 367814976 | bytes 14738400 | tf_op jit(solution)/shard_map/ihqk,iqhd->ikhd/dot_general | solution.py:148
  600.0 11.2 %multiply_reduce_fusion = (f32[24,3,196]{2,1,0:T(4,128)S(1)}, f32[24,3,196,196]{2,3,1,0:T(8,128)}) fusion(f32[24,3,196,196]{2,3,1,0:T(8,128)S(1)} %bitcast.79, f32[24,3,196]{2,1,0:T(4,128)S(1)} %copy-done.24, pred[24,196]{1,0:T(8,128)(4,1)S(1)} %copy-done.30, f32[24,196,3,64]{1,0,3,2:T(8,128)} %squeeze.8, f32[3,64]{1,0:T(4,128)S(1)} %copy-done.47, ...), kind=kOutput, calls=%fused_computation.2 | convolution fusion | flops 369663840 | bytes 27664992 | tf_op jit(solution)/shard_map/iqhd,ikhd->ihqk/dot_general | solution.py:151
  611.1 10.4 %multiply_convert_fusion = bf16[24,3,196,196]{2,3,1,0:T(8,128)(2,1)} fusion(f32[24,3,196,196]{2,3,1,0:T(8,128)} %get-tuple-element.59, f32[24,3,196,196]{2,3,1,0:T(8,128)S(1)} %bitcast.79, f32[24,3,196]{2,1,0:T(4,128)S(1)} %get-tuple-element.58, f32[24,3,196]{2,1,0:T(4,128)S(1)} %copy-done.24, pred[24,196]{1,0:T(8,128)(4,1)S(1)} %copy-done.30), kind=kLoop, calls=%fused_computation.1 | loop fusion | flops 16595712 | bytes 27777120 | tf_op jit(solution)/shard_map/convert_element_type | solution.py:155
  621.6 8.7 fusion.43
  630.3 2.9 convert_reduce_fusion.4
  633.3 2.8 copy.53
  636.1 4.7 convert_element_type.185
  643.6 4.7 convert_element_type.179
  648.3 3.0 copy.50
  651.3 3.0 convert_element_type.182
  659.5 7.9 bitcast_convert_fusion
  667.5 11.7 %fusion.38 = f32[768,768]{1,0:T(8,128)} fusion(bf16[4704,768]{1,0:T(8,128)(2,1)} %all-gather.7.cloned.1.call-done, bf16[4704,768]{1,0:T(8,128)(2,1)} %get-tuple-element.43), kind=kOutput, calls=%fused_computation.78 | convolution fusion | flops 5549064192 | bytes 16809984 | tf_op jit(solution)/shard_map/td,tf->df/dot_general | solution.py:119
  679.2 12.2 %fusion.76 = f32[768,768]{1,0:T(8,128)} fusion(bf16[4704,768]{1,0:T(8,128)(2,1)} %multiply_convert_fusion.1, bf16[4704,768]{1,0:T(8,128)(2,1)} %all-gather.9.cloned.1.call-done), kind=kOutput, calls=%fused_computation.134 | convolution fusion | flops 5549064192 | bytes 16809984 | tf_op jit(solution)/shard_map/tf,td->fd/dot_general | solution.py:113
  693.9 5.9 fusion.8
  699.9 2.8 pad_maximum_fusion.1
  702.9 22.3 %all-reduce.1 = (f32[2,192]{1,0:T(2,128)}, f32[768]{0:T(1024)}) all-reduce(f32[2,192]{1,0:T(2,128)S(1)} %pad_maximum_fusion, f32[768]{0:T(1024)S(1)} %get-tuple-element.42), channel_id=1, replica_groups=mesh['dp'=8,'tensor'=4] {'dp'}, use_global_device_ids=true, to_apply=%region_22.23 | all-reduce | flops 1152 | bytes 9216 | tf_op jit(solution)/shard_map/psum | solution.py:207
  725.1 7.6 reduce-scatter.11.cloned.1.call-done
  732.7 3.4 fusion.37
  736.2 44.5 %all-reduce = (f32[768]{0:T(1024)}, f32[768]{0:T(1024)}, f32[768]{0:T(1024)}, f32[768]{0:T(1024)}, f32[768]{0:T(1024)}, /*index=5*/f32[768]{0:T(1024)}, f32[4]{0:T(128)S(1)}) all-reduce(f32[768]{0:T(1024)S(1)} %get-tuple-element.17, f32[768]{0:T(1024)S(1)} %get-tuple-element.25, ...), channel_id=1, replica_groups=mesh['dp'=8,'tensor'=4] {'dp','tensor'}, use_global_device_ids=true, to_apply=%region_16.17 | all-reduce | flops 4612 | bytes 36896 | tf_op jit(solution)/shard_map/psum | solution.py:195
  782.4 4.6 fusion.29
  787.0 183.9 %all-reduce.5.cloned.1.call-done = (f32[768,3,192]{0,2,1:T(8,128)}, f32[192,768]{1,0:T(8,128)}, f32[768,768]{1,0:T(8,128)}, f32[768,768]{1,0:T(8,128)}) async-done(((f32[768,3,192]{0,2,1:T(8,128)}, f32[192,768]{1,0:T(8,128)}, f32[768,768]{1,0:T(8,128)}, f32[768,768]{1,0:T(8,128)}), (f32[768,3,192]{0,2,1:T(8,128)}, f32[192,768]{1,0:T(8,128)}, f32[768,768]{1,0:T(8,128)}, ...) | async-done | bytes 7077904 | tf_op jit(solution)/shard_map/psum | solution.py:207
  971.0 2.9 copy.96
  (194 shorter events, 48.1 us)
Async XLA Ops:
  7.2 313.2 %copy-start = (bf16[768,768]{1,0:T(8,128)(2,1)S(1)}, bf16[768,768]{1,0:T(8,128)(2,1)}, u32[]{:S(2)}) copy-start(bf16[768,768]{1,0:T(8,128)(2,1)} %param.27) | copy-start | bytes 3538948
  7.2 8.9 copy-start.56
  7.2 62.0 %all-gather.5.cloned.1.call-start = ((), (), s32[]{:S(2)}) async-start(), calls=%async_computation.4 | async-start | bytes 9031680 | tf_op jit(solution)/shard_map/all_gather | solution.py:68
  14.7 189.6 %reduce-scatter.5.cloned.1.call-start = ((), (), s32[]{:S(2)}) async-start(), calls=%async_computation.5 | async-start | bytes 9031680 | tf_op jit(solution)/shard_map/reduce_scatter | solution.py:84
  16.8 97.0 %copy-start.29 = (pred[24,196]{1,0:T(8,128)(4,1)}, pred[24,196]{1,0:T(8,128)(4,1)S(1)}, u32[]{:S(2)}) copy-start(pred[24,196]{1,0:T(8,128)(4,1)S(1)} %get-tuple-element.54) | copy-start | bytes 14116
  113.8 11.1 %copy-start.23 = (f32[24,3,196]{2,1,0:T(4,128)}, f32[24,3,196]{2,1,0:T(4,128)S(1)}, u32[]{:S(2)}) copy-start(f32[24,3,196]{2,1,0:T(4,128)S(1)} %log_add_fusion) | copy-start | bytes 169348
  138.9 65.4 %copy-start.41 = (f32[768]{0:T(1024)S(1)}, f32[768]{0:T(1024)}, u32[]{:S(2)}) copy-start(f32[768]{0:T(1024)} %param.22) | copy-start | bytes 9220
  139.0 127.7 %all-gather.7.cloned.1.call-start = ((), (), s32[]{:S(2)}) async-start(), calls=%async_computation.6 | async-start | bytes 9031680 | tf_op jit(solution)/shard_map/all_gather | solution.py:95
  140.5 71.5 %copy-start.37 = (f32[1176]{0:T(1024)}, f32[1176]{0:T(1024)S(1)}, u32[]{:S(2)}) copy-start(f32[1176]{0:T(1024)S(1)} %get-tuple-element.46) | copy-start | bytes 14116
  140.5 72.2 %copy-start.44 = (f32[768]{0:T(1024)S(1)}, f32[768]{0:T(1024)}, u32[]{:S(2)}) copy-start(f32[768]{0:T(1024)} %param.23) | copy-start | bytes 9220
  140.5 72.2 %copy-start.52 = (f32[768]{0:T(1024)S(1)}, f32[768]{0:T(1024)}, u32[]{:S(2)}) copy-start(f32[768]{0:T(1024)} %param.24) | copy-start | bytes 9220
  214.9 105.5 %all-gather.9.cloned.1.call-start = ((), (), s32[]{:S(2)}) async-start(), calls=%async_computation.8 | async-start | bytes 9031680 | tf_op jit(solution)/shard_map/all_gather | solution.py:112
  215.5 104.9 %copy-start.50 = (f32[768]{0:T(1024)S(1)}, f32[768]{0:T(1024)}, u32[]{:S(2)}) copy-start(f32[768]{0:T(1024)} %param.26) | copy-start | bytes 9220
  215.5 226.5 %reduce-scatter.7.cloned.1.call-start = ((), (), s32[]{:S(2)}) async-start(), calls=%async_computation.7 | async-start | bytes 9031680 | tf_op jit(solution)/shard_map/reduce_scatter | solution.py:100
  320.4 41.1 %copy-start.13 = (f32[4704,768]{1,0:T(8,128)S(1)}, f32[4704,768]{1,0:T(8,128)}, u32[]{:S(2)}) copy-start(f32[4704,768]{1,0:T(8,128)} %fusion.74) | copy-start | bytes 43352068
  376.6 132.9 %reduce-scatter.9.cloned.1.call-start = ((), (), s32[]{:S(2)}) async-start(), calls=%async_computation.9 | async-start | bytes 9031680 | tf_op jit(solution)/shard_map/reduce_scatter | solution.py:121
  388.9 120.7 %copy-start.4 = (bf16[1176,768]{1,0:T(8,128)(2,1)S(1)}, bf16[1176,768]{1,0:T(8,128)(2,1)}, u32[]{:S(2)}) copy-start(bf16[1176,768]{1,0:T(8,128)(2,1)} %param.15) | copy-start | bytes 5419012
  388.9 120.7 %copy-start.34 = (f32[1176]{0:T(1024)S(1)}, f32[1176]{0:T(1024)}, u32[]{:S(2)}) copy-start(f32[1176]{0:T(1024)} %copy-done.33) | copy-start | bytes 14116
  388.9 120.7 %copy-start.38 = (f32[1176]{0:T(1024)S(1)}, f32[1176]{0:T(1024)}, u32[]{:S(2)}) copy-start(f32[1176]{0:T(1024)} %copy-done.37) | copy-start | bytes 14116
  388.9 120.7 %copy-start.40 = (f32[1176]{0:T(1024)S(1)}, f32[1176]{0:T(1024)}, u32[]{:S(2)}) copy-start(f32[1176]{0:T(1024)} %copy-done.39) | copy-start | bytes 14116
  388.9 120.7 %copy-start.42 = (f32[768]{0:T(1024)S(1)}, f32[768]{0:T(1024)}, u32[]{:S(2)}) copy-start(f32[768]{0:T(1024)} %param.22) | copy-start | bytes 9220
  388.9 120.7 %copy-start.45 = (f32[768]{0:T(1024)S(1)}, f32[768]{0:T(1024)}, u32[]{:S(2)}) copy-start(f32[768]{0:T(1024)} %param.23) | copy-start | bytes 9220
  388.9 120.7 %copy-start.51 = (f32[768]{0:T(1024)S(1)}, f32[768]{0:T(1024)}, u32[]{:S(2)}) copy-start(f32[768]{0:T(1024)} %param.28) | copy-start | bytes 9220
  389.0 186.4 %all-gather.11.cloned.1.call-start = ((), (), s32[]{:S(2)}) async-start(), calls=%async_computation.10 | async-start | bytes 9031680 | tf_op jit(solution)/shard_map/all_gather | solution.py:133
  520.3 55.1 %copy-start.28 = (bf16[192,768]{1,0:T(8,128)(2,1)S(1)}, bf16[192,768]{1,0:T(8,128)(2,1)}, u32[]{:S(2)}) copy-start(bf16[192,768]{1,0:T(8,128)(2,1)} %param.21) | copy-start | bytes 884740
  523.5 64.9 %copy-start.24 = (f32[24,3,196]{2,1,0:T(4,128)S(1)}, f32[24,3,196]{2,1,0:T(4,128)}, u32[]{:S(2)}) copy-start(f32[24,3,196]{2,1,0:T(4,128)} %copy-done.23) | copy-start | bytes 169348
  523.6 64.8 %copy-start.30 = (pred[24,196]{1,0:T(8,128)(4,1)S(1)}, pred[24,196]{1,0:T(8,128)(4,1)}, u32[]{:S(2)}) copy-start(pred[24,196]{1,0:T(8,128)(4,1)} %copy-done.29) | copy-start | bytes 14116
  523.6 209.2 %reduce-scatter.11.cloned.1.call-start = ((), (), s32[]{:S(2)}) async-start(), calls=%async_computation.11 | async-start | bytes 9031680 | tf_op jit(solution)/shard_map/reduce_scatter | solution.py:176
  582.2 16.2 %slice-start = ((s8[14745600]{0:T(1024)(128)(4,1)}), s8[2162688]{0:T(1024)(128)(4,1)S(1)}, s32[]{:S(2)}) async-start(s8[14745600]{0:T(1024)(128)(4,1)} %bitcast.78), calls=%async_computation.13 | async-start | bytes 4325376
  588.4 10.0 %slice-start.1 = ((s8[14745600]{0:T(1024)(128)(4,1)}), s8[4194304]{0:T(1024)(128)(4,1)S(1)}, s32[]{:S(2)}) async-start(s8[14745600]{0:T(1024)(128)(4,1)} %bitcast.78), calls=%async_computation.14 | async-start | bytes 8388608
  588.4 10.0 %slice-start.2 = ((s8[14745600]{0:T(1024)(128)(4,1)}), s8[4194304]{0:T(1024)(128)(4,1)S(1)}, s32[]{:S(2)}) async-start(s8[14745600]{0:T(1024)(128)(4,1)} %bitcast.78), calls=%async_computation.15 | async-start | bytes 8388608
  588.4 10.9 %slice-start.3 = ((s8[14745600]{0:T(1024)(128)(4,1)}), s8[4194304]{0:T(1024)(128)(4,1)S(1)}, s32[]{:S(2)}) async-start(s8[14745600]{0:T(1024)(128)(4,1)} %bitcast.78), calls=%async_computation.16 | async-start | bytes 8388608
  588.4 11.5 %copy-start.11 = (bf16[24,196,3,64]{1,0,3,2:T(8,128)(2,1)S(1)}, bf16[24,196,3,64]{1,0,3,2:T(8,128)(2,1)}, u32[]{:S(2)}) copy-start(bf16[24,196,3,64]{1,0,3,2:T(8,128)(2,1)} %reshape.193) | copy-start | bytes 5419012
  588.4 11.5 %copy-start.47 = (f32[3,64]{1,0:T(4,128)S(1)}, f32[3,64]{1,0:T(4,128)}, u32[]{:S(2)}) copy-start(f32[3,64]{1,0:T(4,128)} %add.138) | copy-start | bytes 2308
  611.1 10.4 %copy-start.48 = (f32[3,64]{1,0:T(4,128)S(1)}, f32[3,64]{1,0:T(4,128)}, u32[]{:S(2)}) copy-start(f32[3,64]{1,0:T(4,128)} %add.141) | copy-start | bytes 2308
  667.4 303.6 %all-reduce.5.cloned.1.call-start = ((), (), s32[]{:S(2)}) async-start(), calls=%async_computation.12 | async-start | bytes 14155776 | tf_op jit(solution)/shard_map/psum | solution.py:207
  667.5 23.9 %slice-start.8 = ((s8[7225344]{0:T(1024)(128)(4,1)}), s8[4194304]{0:T(1024)(128)(4,1)S(1)}, s32[]{:S(2)}) async-start(s8[7225344]{0:T(1024)(128)(4,1)} %bitcast.86), calls=%async_computation.21 | async-start | bytes 8388608
  667.5 26.5 %slice-start.4 = ((s8[5455872]{0:T(1024)(128)(4,1)}), s8[4194304]{0:T(1024)(128)(4,1)S(1)}, s32[]{:S(2)}) async-start(s8[5455872]{0:T(1024)(128)(4,1)} %bitcast.82), calls=%async_computation.17 | async-start | bytes 8388608
  667.5 26.4 %slice-start.6 = ((s8[7225344]{0:T(1024)(128)(4,1)}), s8[4194304]{0:T(1024)(128)(4,1)S(1)}, s32[]{:S(2)}) async-start(s8[7225344]{0:T(1024)(128)(4,1)} %bitcast.84), calls=%async_computation.19 | async-start | bytes 8388608
  679.2 12.2 %copy-start.14 = (bf16[4704,192]{0,1:T(8,128)(2,1)S(1)}, bf16[4704,192]{0,1:T(8,128)(2,1)}, u32[]{:S(2)}) copy-start(bf16[4704,192]{0,1:T(8,128)(2,1)} %convert_element_type.159) | copy-start | bytes 5419012
  679.2 12.2 %slice-start.9 = ((s8[7225344]{0:T(1024)(128)(4,1)}), s8[3031040]{0:T(1024)(128)(4,1)S(1)}, s32[]{:S(2)}) async-start(s8[7225344]{0:T(1024)(128)(4,1)} %bitcast.86), calls=%async_computation.22 | async-start | bytes 6062080
  679.2 14.7 %slice-start.5 = ((s8[5455872]{0:T(1024)(128)(4,1)}), s8[1261568]{0:T(1024)(128)(4,1)S(1)}, s32[]{:S(2)}) async-start(s8[5455872]{0:T(1024)(128)(4,1)} %bitcast.82), calls=%async_computation.18 | async-start | bytes 2523136
  679.2 14.7 %slice-start.7 = ((s8[7225344]{0:T(1024)(128)(4,1)}), s8[3031040]{0:T(1024)(128)(4,1)S(1)}, s32[]{:S(2)}) async-start(s8[7225344]{0:T(1024)(128)(4,1)} %bitcast.84), calls=%async_computation.20 | async-start | bytes 6062080
  699.9 32.9 %copy-start.5 = (bf16[1176,768]{1,0:T(8,128)(2,1)S(1)}, bf16[1176,768]{1,0:T(8,128)(2,1)}, u32[]{:S(2)}) copy-start(bf16[1176,768]{1,0:T(8,128)(2,1)} %param.15) | copy-start | bytes 5419012
  699.9 32.9 %copy-start.32 = (f32[1176]{0:T(1024)S(1)}, f32[1176]{0:T(1024)}, u32[]{:S(2)}) copy-start(f32[1176]{0:T(1024)} %copy-done.31) | copy-start | bytes 14116
  699.9 32.9 %copy-start.36 = (f32[1176]{0:T(1024)S(1)}, f32[1176]{0:T(1024)}, u32[]{:S(2)}) copy-start(f32[1176]{0:T(1024)} %copy-done.35) | copy-start | bytes 14116
  699.9 32.9 %copy-start.46 = (f32[768]{0:T(1024)S(1)}, f32[768]{0:T(1024)}, u32[]{:S(2)}) copy-start(f32[768]{0:T(1024)} %param.17) | copy-start | bytes 9220
  699.9 36.3 %copy-start.49 = (f32[768]{0:T(1024)S(1)}, f32[768]{0:T(1024)}, u32[]{:S(2)}) copy-start(f32[768]{0:T(1024)} %get-tuple-element.26) | copy-start | bytes 9220
  (28 other events, 124.4 us)
Sparse Core Ops, SparseCore 0:
  14.8 54.3 all-gather.4
  139.1 65.1 reduce-scatter.4
  215.0 51.6 all-gather.6
  268.7 51.6 all-gather.8
  376.8 65.1 reduce-scatter.6
  444.4 65.1 reduce-scatter.8
  523.7 51.6 all-gather.10
  667.5 65.1 reduce-scatter.10
  738.3 232.6 all-reduce.4
where the time goes:
time: 995 us; the launch traced here: 985 us
  waiting for transfers between devices  574 us (58%)
  matrix products  187 us (19%)
  local copies, waits for them, and re-layouts  81.2 us (8%)
  blocking collectives  66.7 us (7%)
  other arithmetic  61.3 us (6%)
  between operations  15.3 us (2%)
    psum x1, waiting for transfers between devices, on_device(): lax.psum((weight_qkv, grad_bias_qv, weight_out, weight_up, grad_bias_up,...  184 us
    reduce_scatter x1, waiting for transfers between devices, on_device(): lax.psum_scatter(jnp.einsum('tf,df->td', piece, w_up, preferred_element_t...  67.6 us
    reduce_scatter x1, waiting for transfers between devices, on_device(): lax.psum_scatter(jnp.dot(piece, w_out, preferred_element_type=jnp.float32...  63.8 us
    reduce_scatter x1, waiting for transfers between devices, on_device(): lax.psum_scatter(jnp.dot(piece, w_down, preferred_element_type=jnp.float3...  53 us
    all_gather x1, waiting for transfers between devices, on_device(): full_attn = lax.all_gather(in_attn, 'tensor', axis=0, tiled=True)  52.4 us
    all_gather x1, waiting for transfers between devices, on_device(): lax.all_gather(grad_hidden.astype(jnp.bfloat16), 'tensor', axis=0, tiled=...  51.8 us
    all_gather x1, waiting for transfers between devices, on_device(): full_mlp = lax.all_gather(in_mlp, 'tensor', axis=0, tiled=True)  51.2 us
    psum x1, blocking collectives, on_device(): lax.psum((grad_gain_attn, grad_shift_attn, grad_bias_out, grad_gain_mlp,...  44.5 us
  transfers between devices with their start and end apart: 9, of which 9 were waited for; matrix products, arithmetic and copies ran while one was open for 7% of the time, Pallas kernels for 0%

commit v1 on v0

v1 whole, which is shorter than its diff:
```python
import jax
import jax.numpy as jnp
from jax import lax
from jax.sharding import PartitionSpec as P

HEAD_DIM = 64
PATCHES = 196
PATCHES_LOW = 144
EPS = 1e-06
F32 = jnp.float32
BF16 = jnp.bfloat16


def normalize(values):
    mean = jnp.mean(values, axis=-1, keepdims=True)
    centred = values - mean
    factor = lax.rsqrt(jnp.mean(centred * centred, axis=-1, keepdims=True) + EPS)
    return (centred * factor, factor)


def norm_back(grad_out, gain, normed, factor):
    scaled = grad_out * gain
    return factor * (
        scaled
        - jnp.mean(scaled, axis=-1, keepdims=True)
        - normed * jnp.mean(scaled * normed, axis=-1, keepdims=True)
    )


def dot(a, b, dims):
    return lax.dot_general(a, b, (dims, ((), ())), preferred_element_type=F32)


NN = ((1,), (0,))
NT = ((1,), (1,))
TN = ((0,), (0,))


def on_device(
    tokens,
    res_class,
    gain_attn,
    shift_attn,
    w_qkv,
    bias_qv,
    w_out,
    bias_out,
    gain_mlp,
    shift_mlp,
    w_up,
    bias_up,
    w_down,
    bias_down,
    cotangent,
):
    rows, width = tokens.shape
    local = w_qkv.shape[2]
    images = rows // PATCHES
    parts = lax.axis_size("tensor")
    heads_here = local // HEAD_DIM
    heads = parts * heads_here
    scale = HEAD_DIM ** (-0.5)
    place = lax.axis_index("tensor")
    ff_local = w_up.shape[1]

    gather = lambda v: lax.all_gather(v, "tensor", axis=0, tiled=False)
    full_qkv = gather(w_qkv.reshape(width, 3 * local))
    full_out = gather(w_out)
    full_up = gather(w_up)
    full_down = gather(w_down)
    bias_q_full = gather(jnp.concatenate([bias_qv[0], bias_qv[1], bias_up]))
    bq = bias_q_full[:, :local]
    bv = bias_q_full[:, local : 2 * local]
    bu = bias_q_full[:, 2 * local :]

    classes = lax.dynamic_slice_in_dim(res_class, place * images, images)
    counts = jnp.where(classes == 0, PATCHES, PATCHES_LOW)
    key_valid = jnp.arange(PATCHES)[None, :] < counts[:, None]
    row_valid = key_valid.reshape(-1).astype(F32)[:, None]
    mask = key_valid[:, None, None, :]

    inputs = tokens.astype(F32)
    normed_a, factor_a = normalize(inputs)
    in_attn = (normed_a * gain_attn + shift_attn).astype(BF16)
    shape = (images, PATCHES, heads_here, HEAD_DIM)
    saved = []
    context = []
    for s in range(parts):
        qkv = dot(in_attn, full_qkv[s], NN)
        query = (qkv[:, :local] + bq[s]).astype(BF16).reshape(shape)
        keys = qkv[:, local : 2 * local].astype(BF16).reshape(shape)
        values = (qkv[:, 2 * local :] + bv[s]).astype(BF16).reshape(shape)
        scores = jnp.einsum("iqhd,ikhd->ihqk", query, keys, preferred_element_type=F32) * scale
        scores = jnp.where(mask, scores, -1e30)
        log_total = jax.nn.logsumexp(scores, axis=-1, keepdims=True)
        probs = jnp.exp(scores - log_total).astype(BF16)
        part = jnp.einsum("ihqk,ikhd->iqhd", probs, values, preferred_element_type=F32)
        context.append(part.reshape(-1, local).astype(BF16))
        saved.append((query, keys, values, probs))
    branch = sum(dot(context[s], full_out[s], NN) for s in range(parts)) + bias_out
    hidden = inputs + branch
    normed_m, factor_m = normalize(hidden)
    in_mlp = (normed_m * gain_mlp + shift_mlp).astype(BF16)
    acts = []
    slopes = []
    mlp = bias_down
    for s in range(parts):
        pre = dot(in_mlp, full_up[s], NN) + bu[s]
        cdf = 0.5 * (1.0 + lax.erf(pre * (2.0 ** -0.5)))
        acts.append((pre * cdf).astype(BF16))
        slopes.append((cdf + pre * jnp.exp(-0.5 * pre * pre) * 0.3989422804014327).astype(BF16))
        mlp = mlp + dot(acts[s], full_down[s], NN)
    stream = (hidden + mlp) * row_valid
    block_out = stream.astype(BF16)

    grad_stream = cotangent.astype(F32) * row_valid
    grad_low = grad_stream.astype(BF16)
    grad_bias_down = jnp.sum(grad_stream, axis=0)
    weight_down, weight_up, grad_bias_up = [], [], []
    grad_in_mlp = 0.0
    for s in range(parts):
        grad_pre = dot(grad_low, full_down[s], NT) * slopes[s].astype(F32)
        grad_bias_up.append(jnp.sum(grad_pre, axis=0))
        grad_pre_low = grad_pre.astype(BF16)
        weight_down.append(dot(acts[s], grad_low, TN).astype(BF16))
        weight_up.append(dot(in_mlp, grad_pre_low, TN).astype(BF16))
        grad_in_mlp = grad_in_mlp + dot(grad_pre_low, full_up[s], NT)
    grad_gain_mlp = jnp.sum(grad_in_mlp * normed_m, axis=0)
    grad_shift_mlp = jnp.sum(grad_in_mlp, axis=0)
    grad_hidden = grad_stream + norm_back(grad_in_mlp, gain_mlp, normed_m, factor_m)
    grad_bias_out = jnp.sum(grad_hidden, axis=0)
    grad_branch = grad_hidden.astype(BF16)

    scatter = lambda v: lax.psum_scatter(v, "tensor", scatter_dimension=0, tiled=False)
    w_mlp = scatter(jnp.stack([jnp.concatenate([u, d], 0) for u, d in zip(weight_up, weight_down)]))
    w_mlp = lax.psum(w_mlp, "dp")

    weight_out, weight_qkv, bias_grads = [], [], []
    grad_in_attn = 0.0
    for s in range(parts):
        query, keys, values, probs = saved[s]
        weight_out.append(dot(context[s], grad_branch, TN).astype(BF16))
        grad_context = dot(grad_branch, full_out[s], NT).astype(BF16).reshape(shape)
        grad_value = jnp.einsum(
            "ihqk,iqhd->ikhd", probs, grad_context, preferred_element_type=F32
        )
        grad_probs = jnp.einsum(
            "iqhd,ikhd->ihqk", grad_context, values, preferred_element_type=F32
        )
        probs_full = probs.astype(F32)
        row_dot = jnp.sum(probs_full * grad_probs, axis=-1, keepdims=True)
        grad_scores = (probs_full * (grad_probs - row_dot)).astype(BF16)
        grad_query = scale * jnp.einsum(
            "ihqk,ikhd->iqhd", grad_scores, keys, preferred_element_type=F32
        )
        grad_key = scale * jnp.einsum(
            "ihqk,iqhd->ikhd", grad_scores, query, preferred_element_type=F32
        )
        low = jnp.concatenate(
            [g.reshape(-1, local).astype(BF16) for g in (grad_query, grad_key, grad_value)], axis=1
        )
        bias_grads.append(jnp.sum(low.astype(F32), axis=0))
        weight_qkv.append(dot(in_attn, low, TN).astype(BF16))
        grad_in_attn = grad_in_attn + dot(low, full_qkv[s], NT)
    w_out_g = scatter(jnp.stack(weight_out))
    w_qkv_g = scatter(jnp.stack(weight_qkv))
    w_out_g, w_qkv_g = lax.psum((w_out_g, w_qkv_g), "dp")
    grad_gain_attn = jnp.sum(grad_in_attn * normed_a, axis=0)
    grad_shift_attn = jnp.sum(grad_in_attn, axis=0)
    grad_tokens = grad_hidden + norm_back(grad_in_attn, gain_attn, normed_a, factor_a)
    totals = jnp.stack(
        [
            jnp.sum(stream * stream),
            jnp.sum(branch * branch * row_valid),
            jnp.sum(mlp * mlp * row_valid),
            jnp.sum(row_valid),
        ]
    )
    pieces = [
        grad_gain_attn,
        grad_shift_attn,
        grad_bias_out,
        grad_gain_mlp,
        grad_shift_mlp,
        grad_bias_down,
        jnp.stack([b[:local] for b in bias_grads]).reshape(-1),
        jnp.stack([b[2 * local :] for b in bias_grads]).reshape(-1),
        jnp.concatenate(grad_bias_up),
        totals,
    ]
    summed = lax.psum(jnp.concatenate(pieces), ("dp", "tensor"))
    got = []
    at = 0
    for p in pieces:
        got.append(summed[at : at + p.shape[0]])
        at += p.shape[0]
    mine = lambda v, n: lax.dynamic_slice_in_dim(v, place * n, n)
    sums = got[9]
    rms = jnp.sqrt(sums[:3] / (sums[3] * width))
    return (
        block_out,
        grad_tokens,
        got[0],
        got[1],
        w_qkv_g.astype(F32).reshape(width, 3, local),
        jnp.stack([mine(got[6], local), mine(got[7], local)]),
        w_out_g.astype(F32),
        got[2],
        got[3],
        got[4],
        w_mlp[:width].astype(F32),
        mine(got[8], ff_local),
        w_mlp[width:].astype(F32),
        got[5],
        rms,
    )


def solution(mesh):
    row = P(("dp", "tensor"), None)
    in_specs = (
        row, P("dp"), P(), P(), P(None, None, "tensor"), P(None, "tensor"), P("tensor", None),
        P(), P(), P(), P(None, "tensor"), P("tensor"), P("tensor", None), P(), row,
    )
    out_specs = (
        row, row, P(), P(), P(None, None, "tensor"), P(None, "tensor"), P("tensor", None),
        P(), P(), P(), P(None, "tensor"), P("tensor"), P("tensor", None), P(), P(),
    )
    return jax.shard_map(
        on_device, mesh=mesh, in_specs=in_specs, out_specs=out_specs, check_vma=False
    )
```

time: 995 us -> 617 us (0.62)
  waiting for transfers between devices: 574 us -> 188 us
  local copies, waits for them, and re-layouts: 81.2 us -> 125 us
  blocking collectives: 66.7 us -> 49.3 us
  matrix products: 187 us -> 171 us
    all_gather x4, waiting for transfers between devices: 197 us -> 22.9 us  [on_device(): gather = lambda v: lax.all_gather(v, 'tensor', axis=0, tiled=False)]
    reduce_scatter x4 -> x3, waiting for transfers between devices: 192 us -> 83.4 us  [on_device(): lax.psum_scatter(v, 'tensor', scatter_dimension=0, tiled=False)]
    psum x1, waiting for transfers between devices: 184 us -> 78.6 us  [on_device(): w_out_g, w_qkv_g = lax.psum((w_out_g, w_qkv_g), 'dp')]
    psum x2 -> x1, blocking collectives: 66.7 us -> 43 us  [on_device(): summed = lax.psum(jnp.concatenate(pieces), ('dp', 'tensor'))]
    reshape x1 -> x18, local copies, waits for them, and re-layouts: 6.2 us -> 28.8 us  [the longest x4 10.5 us: on_device(): grad_context = dot(grad_branch, full_out[s], NT).astype(BF16).reshape(shape)]
    convert_element_type x10 -> x33, local copies, waits for them, and re-layouts: 34.7 us -> 50.3 us  [the longest x24 37 us: on_device(): g.reshape(-1, local).astype(BF16)]
    unnamed x140 -> x228, local copies, waits for them, and re-layouts: 20.2 us -> 35 us
    reduce_sum x3 -> x4, other arithmetic: 16.8 us -> 2.53 us  [on_device(): bias_grads.append(jnp.sum(low.astype(F32), axis=0))]
  transfers between devices with their start and end apart: 9 -> 8, of which waited for: 9 -> 4; matrix products, arithmetic and copies ran while one was open for 7% -> 30% of each run, Pallas kernels for 0% -> 0%
where the time goes in v1:
time: 617 us; the launch traced here: 608 us
  waiting for transfers between devices  188 us (30%)
  matrix products  171 us (28%)
  local copies, waits for them, and re-layouts  125 us (20%)
  other arithmetic  57.2 us (9%)
  blocking collectives  49.3 us (8%)
  between operations  16.6 us (3%)
    dot_general x48, matrix products, dot(): return lax.dot_general(a, b, (dims, ((), ())), preferred_element_type=F32)  127 us
    reduce_scatter x3, waiting for transfers between devices, on_device(): lax.psum_scatter(v, 'tensor', scatter_dimension=0, tiled=False)  83.4 us
    psum x1, waiting for transfers between devices, on_device(): w_out_g, w_qkv_g = lax.psum((w_out_g, w_qkv_g), 'dp')  78.6 us
    psum x1, blocking collectives, on_device(): summed = lax.psum(jnp.concatenate(pieces), ('dp', 'tensor'))  43 us
    convert_element_type x24, local copies, waits for them, and re-layouts, on_device(): g.reshape(-1, local).astype(BF16)  37 us
    unnamed x228, local copies, waits for them, and re-layouts  35 us
    all_gather x4, waiting for transfers between devices, on_device(): gather = lambda v: lax.all_gather(v, 'tensor', axis=0, tiled=False)  22.9 us
    convert_element_type x8, local copies, waits for them, and re-layouts, on_device(): context.append(part.reshape(-1, local).astype(BF16))  13.3 us
  transfers between devices with their start and end apart: 8, of which 4 were waited for; matrix products, arithmetic and copies ran while one was open for 30% of the time, Pallas kernels for 0%

profile of v1, /device:TPU:0, one launch (start us, length us, event | category | flops | bytes accessed | tf_op | source)
XLA Modules:
  0.0 607.9 jit_solution(5200933843008387794)
XLA Ops:
  10.2 6.2 %all-gather.4 = f32[4,1,1152]{2,1,0:T(1,128)S(1)} all-gather(f32[1,1,1152]{2,1,0:T(1,128)S(1)} %reshape.325), channel_id=2, replica_groups=mesh['dp'=8,'tensor'=4] {'tensor'}, dimensions={0}, use_global_device_ids=true | all-gather | bytes 23040 | tf_op jit(solution)/shard_map/all_gather | solution.py:66
  20.3 22.9 %all-gather.10.cloned.1.call-done = bf16[4,768,576]{1,2,0:T(8,128)(2,1)} async-done(((bf16[1,768,576]{1,2,0:T(8,128)(2,1)}), bf16[4,768,576]{1,2,0:T(8,128)(2,1)}) %all-gather.10.cloned.1.call-update) | async-done | bytes 3538960 | tf_op jit(solution)/shard_map/all_gather | solution.py:66
  43.1 3.1 fusion.116
  48.8 2.7 fusion.103
  52.5 3.3 fusion.115
  63.6 3.1 fusion.118
  69.3 3.1 fusion.99
  72.4 2.6 reshape.285
  77.4 3.5 fusion.48
  81.0 2.5 fusion.117
  86.1 2.7 fusion.101
  89.8 8.0 %exponential_reduce_fusion = (f32[6,3,196]{2,1,0:T(4,128)S(1)}, f32[6,3,196]{2,1,0:T(4,128)S(1)}, f32[6,3,196]{2,1,0:T(4,128)S(1)}, f32[6,3,196]{2,1,0:T(4,128)S(1)}, f32[6,3,196,196]{2,3,1,0:T(8,128)}) fusion(f32[6,3,196,196]{2,3,1,0:T(8,128)} %get-tuple-element.91, f32[6,3,196]{2,1,0:T(4,128)S(1)} %get-tuple-element.119, ...), kind=kOutput, calls=%fused_computation.53 | convolution fusion | flops 98868672 | bytes 12066936 | tf_op jit(solution)/shard_map/iqhd,ikhd->ihqk/dot_general | solution.py:93
  98.8 3.3 exponential_reduce_fusion.1
  102.2 7.3 %exponential_convert_fusion = (bf16[6,3,196,196]{2,3,1,0:T(8,128)(2,1)S(1)}, bf16[6,3,196,196]{2,3,1,0:T(8,128)(2,1)S(1)}, bf16[6,3,196,196]{2,3,1,0:T(8,128)(2,1)}, bf16[6,3,196,196]{2,3,1,0:T(8,128)(2,1)}) fusion(f32[6,3,196,196]{2,3,1,0:T(8,128)} %get-tuple-element.91, f32[6,3,196]{2,1,0:T(4,128)S(1)} %log_add_fusion, ...), kind=kLoop, calls=%fused_computation.52 | loop fusion | flops 11063808 | bytes 16653336 | tf_op jit(solution)/shard_map/convert_element_type | solution.py:96
  132.8 2.9 convert_element_type.405
  140.4 2.8 fusion.180
  146.9 6.0 multiply_convert_fusion.3
  152.9 5.6 fusion.188
  160.6 5.0 multiply_convert_fusion.2
  165.6 3.4 fusion.189
  169.0 5.0 multiply_convert_fusion.1
  174.0 3.4 fusion.190
  177.4 4.2 multiply_convert_fusion
  181.6 3.4 fusion.191
  197.1 6.0 multiply_reduce_fusion
  208.1 2.5 convolution_convert_fusion.3
  210.6 2.8 reshape.287
  213.4 2.8 fusion.7
  221.6 2.5 convolution_convert_fusion.2
  224.1 2.7 reshape.288
  226.8 2.8 fusion.9
  237.6 2.7 reshape.289
  240.3 2.8 fusion.11
  282.7 2.6 convert_element_type.461
  319.1 3.4 fusion.60
  329.2 3.9 convolution_convert_fusion.5
  352.6 4.6 pad_maximum_fusion
  361.4 5.1 fusion.114
  366.5 2.9 reduce-scatter.4.cloned.1.call-done
  369.4 80.5 %reduce-scatter.8.cloned.1.call-done = bf16[1,1536,768]{2,1,0:T(8,128)(2,1)} async-done(((bf16[4,1536,768]{2,1,0:T(8,128)(2,1)}), bf16[1,1536,768]{2,1,0:T(8,128)(2,1)}) %reduce-scatter.8.cloned.1.call-update) | async-done | bytes 2359312 | tf_op jit(solution)/shard_map/reduce_scatter | solution.py:134
  450.0 4.1 convolution_add_fusion.5
  456.0 4.6 fusion.21
  460.7 2.7 concatenate.35
  463.3 43.0 %psum.28 = f32[9220]{0:T(1024)S(1)} all-reduce(f32[9220]{0:T(1024)S(1)} %concatenate.35), channel_id=1, replica_groups=mesh['dp'=8,'tensor'=4] {'dp','tensor'}, use_global_device_ids=true, to_apply=%region_38.39 | all-reduce | flops 9220 | bytes 73760 | tf_op jit(solution)/shard_map/psum | solution.py:191
  510.2 5.0 fusion.20
  515.2 78.6 %all-reduce.3.cloned.1.call-done = (bf16[768,3,192]{0,2,1:T(8,128)(2,1)}, bf16[192,768]{1,0:T(8,128)(2,1)}, bf16[1536,768]{1,0:T(8,128)(2,1)}) async-done(((bf16[768,3,192]{0,2,1:T(8,128)(2,1)}, bf16[192,768]{1,0:T(8,128)(2,1)}, bf16[1536,768]{1,0:T(8,128)(2,1)}), (bf16[768,3,192]{0,2,1:T(8,128)(2,1)}, bf16[192,768]{1,0:T(8,128)(2,1)}, bf16[1536,768]{1,0:T(8,128)(2,1)})) %all-reduce.3.cloned.1.call-update) | async-done | bytes 3538960 | tf_op jit(solution)/shard_map/psum | solution.py:167
  593.8 2.7 reshape.294
  598.3 2.5 slice_convert_fusion
  (407 shorter events, 201.5 us)
Async XLA Ops:
  7.2 9.4 %copy-start.91 = (s32[24]{0:T(128)S(1)}, s32[24]{0:T(128)}, u32[]{:S(2)}) copy-start(s32[24]{0:T(128)} %param.16) | copy-start | bytes 292
  7.2 10.0 %copy-start.6 = (bf16[1176,768]{1,0:T(8,128)(2,1)S(1)}, bf16[1176,768]{1,0:T(8,128)(2,1)}, u32[]{:S(2)}) copy-start(bf16[1176,768]{1,0:T(8,128)(2,1)} %param.15) | copy-start | bytes 5419012
  7.2 35.9 %all-gather.10.cloned.1.call-start = ((), (), s32[]{:S(2)}) async-start(), calls=%async_computation.3 | async-start | bytes 4423680 | tf_op jit(solution)/shard_map/all_gather | solution.py:66
  8.0 127.7 %all-gather.12.cloned.1.call-start = ((), (), s32[]{:S(2)}) async-start(), calls=%async_computation.7 | async-start | bytes 1474560 | tf_op jit(solution)/shard_map/all_gather | solution.py:66
  8.7 9.6 %copy-start.76 = (f32[768]{0:T(1024)S(1)}, f32[768]{0:T(1024)}, u32[]{:S(2)}) copy-start(f32[768]{0:T(1024)} %param.17) | copy-start | bytes 9220
  8.7 9.6 %copy-start.78 = (f32[768]{0:T(1024)S(1)}, f32[768]{0:T(1024)}, u32[]{:S(2)}) copy-start(f32[768]{0:T(1024)} %param.18) | copy-start | bytes 9220
  8.7 138.2 %all-gather.14.cloned.1.call-start = ((), (), s32[]{:S(2)}) async-start(), calls=%async_computation.8 | async-start | bytes 5898240 | tf_op jit(solution)/shard_map/all_gather | solution.py:66
  9.5 143.4 %all-gather.16.cloned.1.call-start = ((), (), s32[]{:S(2)}) async-start(), calls=%async_computation.9 | async-start | bytes 5898240 | tf_op jit(solution)/shard_map/all_gather | solution.py:66
  10.0 356.5 %reduce-scatter.6.cloned.1.call-start = ((), (), s32[]{:S(2)}) async-start(), calls=%async_computation.5 | async-start | bytes 1474560 | tf_op jit(solution)/shard_map/reduce_scatter | solution.py:134
  17.6 28.6 %copy-start.71 = (f32[1176]{0:T(1024)}, f32[1176]{0:T(1024)S(1)}, u32[]{:S(2)}) copy-start(f32[1176]{0:T(1024)S(1)} %broadcast_multiply_fusion.5) | copy-start | bytes 14116
  18.3 27.9 %copy-start.73 = (f32[1176]{0:T(1024)}, f32[1176]{0:T(1024)S(1)}, u32[]{:S(2)}) copy-start(f32[1176]{0:T(1024)S(1)} %add_rsqrt_fusion.1) | copy-start | bytes 14116
  48.8 26.2 %copy-start.22 = (bf16[6,196,3,64]{1,0,3,2:T(8,128)(2,1)}, bf16[6,196,3,64]{1,0,3,2:T(8,128)(2,1)S(1)}, u32[]{:S(2)}) copy-start(bf16[6,196,3,64]{1,0,3,2:T(8,128)(2,1)S(1)} %reshape.280) | copy-start | bytes 1354756
  52.5 22.5 %copy-start.24 = (bf16[6,196,3,64]{1,0,3,2:T(8,128)(2,1)}, bf16[6,196,3,64]{1,0,3,2:T(8,128)(2,1)S(1)}, u32[]{:S(2)}) copy-start(bf16[6,196,3,64]{1,0,3,2:T(8,128)(2,1)S(1)} %reshape.279) | copy-start | bytes 1354756
  69.3 8.1 %copy-start.18 = (bf16[6,196,3,64]{1,0,3,2:T(8,128)(2,1)}, bf16[6,196,3,64]{1,0,3,2:T(8,128)(2,1)S(1)}, u32[]{:S(2)}) copy-start(bf16[6,196,3,64]{1,0,3,2:T(8,128)(2,1)S(1)} %reshape.286) | copy-start | bytes 1354756
  76.7 4.2 copy-start.14
  77.4 3.5 copy-start.16
  77.4 3.5 copy-start.65
  86.1 11.7 %copy-start.48 = (bf16[6,196,3,64]{1,0,3,2:T(8,128)(2,1)}, bf16[6,196,3,64]{1,0,3,2:T(8,128)(2,1)S(1)}, u32[]{:S(2)}) copy-start(bf16[6,196,3,64]{1,0,3,2:T(8,128)(2,1)S(1)} %reshape.283) | copy-start | bytes 1354756
  89.8 8.0 %copy-start.50 = (bf16[6,196,3,64]{1,0,3,2:T(8,128)(2,1)}, bf16[6,196,3,64]{1,0,3,2:T(8,128)(2,1)S(1)}, u32[]{:S(2)}) copy-start(bf16[6,196,3,64]{1,0,3,2:T(8,128)(2,1)S(1)} %reshape.282) | copy-start | bytes 1354756
  89.8 8.0 %copy-start.62 = (bf16[1176,192]{0,1:T(8,128)(2,1)S(1)}, bf16[1176,192]{0,1:T(8,128)(2,1)}, u32[]{:S(2)}) copy-start(bf16[1176,192]{0,1:T(8,128)(2,1)} %get-tuple-element.55) | copy-start | bytes 1354756
  115.1 5.9 copy-start.32
  123.1 5.9 copy-start.30
  152.9 5.6 copy-start.89
  158.4 7.1 %slice-start = ((s8[4718592]{0:T(1024)(128)(4,1)}), s8[4194304]{0:T(1024)(128)(4,1)S(1)}, s32[]{:S(2)}) async-start(s8[4718592]{0:T(1024)(128)(4,1)} %bitcast.268), calls=%async_computation.11 | async-start | bytes 8388608
  160.6 5.0 copy-start.63
  160.6 5.0 slice-start.1
  165.6 26.2 %copy-start.92 = (bf16[1176,768]{1,0:T(8,128)(2,1)}, bf16[1176,768]{1,0:T(8,128)(2,1)S(1)}, u32[]{:S(2)}) copy-start(bf16[1176,768]{1,0:T(8,128)(2,1)S(1)} %get-tuple-element.96) | copy-start | bytes 5419012
  169.0 15.9 %copy-start.94 = (bf16[1176,768]{1,0:T(8,128)(2,1)}, bf16[1176,768]{1,0:T(8,128)(2,1)S(1)}, u32[]{:S(2)}) copy-start(bf16[1176,768]{1,0:T(8,128)(2,1)S(1)} %get-tuple-element.114) | copy-start | bytes 5419012
  174.0 19.5 %copy-start.96 = (bf16[1176,768]{1,0:T(8,128)(2,1)}, bf16[1176,768]{1,0:T(8,128)(2,1)S(1)}, u32[]{:S(2)}) copy-start(bf16[1176,768]{1,0:T(8,128)(2,1)S(1)} %get-tuple-element.98) | copy-start | bytes 5419012
  177.4 9.3 %copy-start.98 = (bf16[1176,768]{1,0:T(8,128)(2,1)}, bf16[1176,768]{1,0:T(8,128)(2,1)S(1)}, u32[]{:S(2)}) copy-start(bf16[1176,768]{1,0:T(8,128)(2,1)S(1)} %get-tuple-element.116) | copy-start | bytes 5419012
  184.9 3.5 copy-start.100
  193.5 3.6 copy-start.105
  220.1 6.8 %copy-start.33 = (bf16[6,196,3,64]{1,0,3,2:T(8,128)(2,1)S(1)}, bf16[6,196,3,64]{1,0,3,2:T(8,128)(2,1)}, u32[]{:S(2)}) copy-start(bf16[6,196,3,64]{1,0,3,2:T(8,128)(2,1)} %copy-done.32) | copy-start | bytes 1354756
  233.6 6.8 %copy-start.31 = (bf16[6,196,3,64]{1,0,3,2:T(8,128)(2,1)S(1)}, bf16[6,196,3,64]{1,0,3,2:T(8,128)(2,1)}, u32[]{:S(2)}) copy-start(bf16[6,196,3,64]{1,0,3,2:T(8,128)(2,1)} %copy-done.30) | copy-start | bytes 1354756
  264.2 3.6 copy-start.54
  269.6 5.0 copy-start.57
  298.9 70.5 %reduce-scatter.4.cloned.1.call-start = ((), (), s32[]{:S(2)}) async-start(), calls=%async_computation.4 | async-start | bytes 4423680 | tf_op jit(solution)/shard_map/reduce_scatter | solution.py:134
  299.0 8.1 %copy-start.53 = (bf16[6,196,3,64]{1,3,2,0:T(8,128)(2,1)S(1)}, bf16[6,196,3,64]{1,3,2,0:T(8,128)(2,1)}, u32[]{:S(2)}) copy-start(bf16[6,196,3,64]{1,3,2,0:T(8,128)(2,1)} %fusion.61) | copy-start | bytes 1354756
  328.7 121.2 %reduce-scatter.8.cloned.1.call-start = ((), (), s32[]{:S(2)}) async-start(), calls=%async_computation.6 | async-start | bytes 11796480 | tf_op jit(solution)/shard_map/reduce_scatter | solution.py:134
  329.2 4.0 copy-start.64
  329.2 4.0 copy-start.106
  357.3 236.5 %all-reduce.3.cloned.1.call-start = ((), (), s32[]{:S(2)}) async-start(), calls=%async_computation.10 | async-start | bytes 7077888 | tf_op jit(solution)/shard_map/psum | solution.py:167
  450.0 4.1 copy-start.70
  456.0 4.7 copy-start.82
  456.0 4.7 copy-start.83
  456.0 4.7 copy-start.84
  456.0 4.7 copy-start.85
  593.8 4.5 copy-start.52
  (69 other events, 138.3 us)
Sparse Core Ops, SparseCore 0:
  9.6 33.5 all-gather.9
  44.7 17.3 all-gather.11
  63.7 37.4 all-gather.13
  102.6 37.4 all-gather.15
  299.1 25.6 reduce-scatter.5
  328.8 40.5 reduce-scatter.3
  372.0 77.8 reduce-scatter.7
  453.9 139.8 all-reduce.2
